TPU v7x, 32 devices: a whole 2x2x4 slice. The times are simulated.
32 devices in a mesh: prow: 4 (over y, core), pcol: 8 (over z, x).
Axes of the slice: x: 2, y: 2, z: 4, core: 2. Of those that a mesh axis runs over, the one named last changes fastest.
Arguments:
- tiles: bfloat16 [4, 8, 16, 256, 256], P('prow', 'pcol'), may hold values from -6 to 6
- tile_ids: int32 [4, 8, 16], P('prow', 'pcol'), may hold values from 0 to 127, as said below
- counts: int32 [4, 8], P('prow', 'pcol'), may hold values from 1 to 16, as said below
- pivots: int32 [256], replicated, may hold values from 0 to 16383, as said below
- l_inverse: bfloat16 [256, 256], P(None, 'pcol'), may hold values from -1 to 1, as said below
- u_inverse: bfloat16 [256, 256], P('prow'), may hold values from -0.125 to 0.5, as said below
Outputs:
- factored: bfloat16 [4, 8, 16, 256, 256], P('prow', 'pcol')
Inputs may be any that keep to these rules, and one draw needn't show every extreme that they name: Live slot s of device (p, q) holds local tile row tile_ids[p, q, s] // 8 and local tile column tile_ids[p, q, s] % 8; live codes of one device are distinct, padded slots hold arbitrary codes. Let R be the tile rows I >= 1 with tile (I, 0) held and C the tile columns J >= 1 with tile (0, J) held. Tile (0, 0) is held; on each prow index R takes the last one to 3 local tile rows, on each pcol index C takes the last one to 3 local tile columns, and both most counts are reached on some index. Every tile whose row is 0 or in R and whose column is 0 or in C is held; no other held tile lies in tile row 0, a tile row of R, or tile column 0. `counts`: some device has 16 live slots. Row r of tile row 0 and row pivots[r] change places; pivots[r] is r or a row of a tile row of R, and the values that differ from their r are distinct. `l_inverse`: lower triangular with unit diagonal. `u_inverse`: upper triangular with a positive diagonal.
All inputs are finite; a program needn't handle non-finite values.
Results may differ from a plain program's by a relative error of at most 0.0056.
Values may be sent and summed in bfloat16 or wider, within the bound.
A program may use at most 64 MiB of HBM per device.

v0:
```python
import jax
import jax.numpy as jnp
from jax import lax
from jax.sharding import PartitionSpec as P

TILE_SIDE = 256
LOCAL_ROWS = 16
TILE_SLOTS = 16
LOWER_MOST = 3
UPPER_MOST = 3


def broadcast(value, axis, source):
    kept = jnp.where(lax.axis_index(axis) == source, value, 0).astype(value.dtype)
    return lax.psum(kept, axis)


def pick_rows(tile, rows):
    return tile[rows]


def body(tiles, tile_ids, counts, pivots, l_inverse, u_inverse):
    row_count = lax.axis_size("prow")
    col_count = lax.axis_size("pcol")
    my_row = lax.axis_index("prow")
    my_col = lax.axis_index("pcol")
    grid_cols = LOCAL_ROWS * row_count // col_count
    total_rows = LOCAL_ROWS * row_count * TILE_SIDE
    local = tiles[0, 0]
    codes = tile_ids[0, 0]
    slot_range = jnp.arange(TILE_SLOTS, dtype=jnp.int32)
    alive = slot_range < counts[0, 0]
    loc_row = codes // grid_cols
    loc_col = codes % grid_cols
    glob_row = my_row + row_count * loc_row
    glob_col = my_col + col_count * loc_col
    col_range = jnp.arange(grid_cols, dtype=jnp.int32)
    upper_inv = lax.all_gather(u_inverse, "prow", axis=0, tiled=True)
    lower_inv = lax.all_gather(l_inverse, "pcol", axis=1, tiled=True)
    source_tile = pivots // TILE_SIDE
    source_row = pivots % TILE_SIDE
    gathered = local[:, source_row, :]
    owned = (source_tile[None, :] == glob_row[:, None]) & alive[:, None]
    contrib = jnp.where(owned[:, :, None], gathered, jnp.zeros_like(gathered))
    col_hot = ((loc_col[:, None] == col_range[None, :]) & alive[:, None]).astype(jnp.bfloat16)
    top_flag = (glob_row == 0).astype(jnp.bfloat16)
    top_hot = col_hot * top_flag[:, None]
    flag_part = jnp.sum(
        top_hot.astype(jnp.float32) * (glob_col >= 1).astype(jnp.float32)[:, None], axis=0
    )
    new_part = jnp.einsum("sj,srb->jrb", col_hot, contrib, preferred_element_type=jnp.float32)
    old_part = jnp.einsum("sj,srb->jrb", top_hot, local, preferred_element_type=jnp.float32)
    new_sum, old_sum, flag_sum = (
        lax.psum(new_part.astype(jnp.bfloat16), "prow").astype(jnp.float32),
        lax.psum(old_part.astype(jnp.bfloat16), "prow").astype(jnp.float32),
        lax.psum(flag_part.astype(jnp.bfloat16), "prow").astype(jnp.float32),
    )
    new_top = new_sum.astype(jnp.bfloat16)
    old_top = old_sum.astype(jnp.bfloat16)
    anchor_top = (
        jnp.full((total_rows,), -1, jnp.int32)
        .at[pivots]
        .set(jnp.arange(TILE_SIDE, dtype=jnp.int32))
    )
    row_index = glob_row[:, None] * TILE_SIDE + jnp.arange(TILE_SIDE, dtype=jnp.int32)[None, :]
    anchor = anchor_top[row_index]
    moved = (anchor >= 0) & (glob_row >= 1)[:, None]
    from_top = jax.vmap(pick_rows)(old_top[loc_col], jnp.maximum(anchor, 0))
    swapped = jnp.where(moved[:, :, None], from_top, local)
    primed = jnp.where((glob_row == 0)[:, None, None], new_top[loc_col], swapped)
    panel_mask = alive & (glob_col == 0) & (glob_row >= 1)
    panel_slots = jnp.argsort(jnp.where(panel_mask, 0, 1), stable=True)[:LOWER_MOST]
    panel_valid = panel_mask[panel_slots]
    lower_full = jnp.einsum(
        "kab,bc->kac", primed[panel_slots], upper_inv, preferred_element_type=jnp.float32
    )
    lower_list = jnp.where(panel_valid[:, None, None], lower_full, 0.0).astype(jnp.bfloat16)
    lower_rows = jnp.where(panel_valid, loc_row[panel_slots], -1)
    got_list, got_rows = (broadcast(lower_list, "pcol", 0), broadcast(lower_rows, "pcol", 0))
    row_match = got_rows[None, :] == loc_row[:, None]
    lower_pick = jnp.sum(
        jnp.where(row_match, jnp.arange(LOWER_MOST, dtype=jnp.int32)[None, :], 0), axis=1
    )
    lower_present = jnp.any(row_match, axis=1)
    column_flags = flag_sum > 0.5
    column_order = jnp.argsort(jnp.where(column_flags, 0, 1), stable=True)[:UPPER_MOST]
    upper_valid = column_flags[column_order]
    upper_full = jnp.einsum(
        "ab,kbc->kac", lower_inv, new_top[column_order], preferred_element_type=jnp.float32
    )
    upper_list = jnp.where(upper_valid[:, None, None], upper_full, 0.0).astype(jnp.bfloat16)
    upper_ids = jnp.where(upper_valid, column_order, -1)
    col_match = upper_ids[None, :] == loc_col[:, None]
    upper_pick = jnp.sum(
        jnp.where(col_match, jnp.arange(UPPER_MOST, dtype=jnp.int32)[None, :], 0), axis=1
    )
    upper_present = jnp.any(col_match, axis=1)
    result = jnp.where(alive[:, None, None], primed, jnp.zeros_like(primed))
    upper_mask = alive & (glob_row == 0) & (glob_col >= 1)
    result = jnp.where(upper_mask[:, None, None], upper_list[upper_pick], result)
    result = result.at[panel_slots].set(
        jnp.where(panel_valid[:, None, None], lower_list, result[panel_slots])
    )
    needs = alive & (glob_row >= 1) & (glob_col >= 1) & lower_present & upper_present
    order = jnp.argsort(jnp.where(needs, 0, 1), stable=True)
    needed = jnp.sum(needs.astype(jnp.int32))

    def trailing(current, lower_tile, upper_index):
        product = jnp.dot(lower_tile, upper_list[upper_index], preferred_element_type=jnp.float32)
        return (current.astype(jnp.float32) - product).astype(jnp.bfloat16)

    def own_step(position, held):
        slot = order[position]
        value = trailing(primed[slot], got_list[lower_pick[slot]], upper_pick[slot])
        return held.at[slot].set(value)

    result = lax.fori_loop(0, needed, own_step, result)
    return result[None, None]


def solution(mesh):
    placed = (
        P("prow", "pcol", None, None, None),
        P("prow", "pcol", None),
        P("prow", "pcol"),
        P(),
        P(None, "pcol"),
        P("prow", None),
    )
    return jax.shard_map(
        body,
        mesh=mesh,
        in_specs=placed,
        out_specs=P("prow", "pcol", None, None, None),
        check_vma=False,
    )
```

profile of v0, /device:TPU:0, one launch (start us, length us, event | category | flops | bytes accessed | tf_op | source)
XLA Modules:
  0.0 367.1 jit_solution(17851985653120215926)
XLA Ops:
  7.2 2.9 copy.87
  10.2 2.2 convolution_convert_fusion
  12.8 2.1 gather_fusion.1
  14.9 3.0 fusion.11
  17.9 8.4 %psum.35 = bf16[8]{0:T(256)(128)(2,1)S(1)} all-reduce(bf16[8]{0:T(256)(128)(2,1)S(1)} %multiply_reduce_fusion), channel_id=1, replica_groups=mesh['prow'=4,'pcol'=8] {'prow'}, use_global_device_ids=true, to_apply=%region_1.2 | all-reduce | flops 8 | bytes 32 | tf_op jit(solution)/shard_map/psum | solution.py:56
  26.4 1.0 sort.48
  28.0 1.2 sort.49
  30.6 11.6 %psum.38 = s32[3]{0:T(128)S(1)} all-reduce(s32[3]{0:T(128)S(1)} %broadcast_select_fusion.2), channel_id=1, replica_groups=mesh['prow'=4,'pcol'=8] {'pcol'}, use_global_device_ids=true, to_apply=%region_9.10 | all-reduce | flops 3 | bytes 24 | tf_op jit(solution)/shard_map/psum | solution.py:15
  42.5 1.4 scatter_custom_fusion
  43.9 23.0 %gather_fusion.5 = s32[4096]{0:T(1024)S(1)} fusion(s32[16384]{0:T(1024)S(1)} %scatter_custom_fusion, s32[4096]{0:T(1024)S(1)} %broadcast_clamp_fusion), kind=kCustom, calls=%fused_computation.5 | custom fusion | bytes 49152 | tf_op jit(solution)/shard_map/gather | solution.py:66
  67.3 6.0 %all_gather.7 = bf16[256,256]{1,0:T(8,128)(2,1)S(1)} all-gather(bf16[64,256]{1,0:T(8,128)(2,1)S(1)} %copy-done.4), channel_id=1, replica_groups=mesh['prow'=4,'pcol'=8] {'prow'}, dimensions={0}, use_global_device_ids=true | all-gather | bytes 163840 | tf_op jit(solution)/shard_map/all_gather | solution.py:38
  73.2 30.7 %all_gather.6 = bf16[256,256]{0,1:T(8,128)(2,1)S(1)} all-gather(bf16[256,32]{0,1:T(8,128)(2,1)S(1)} %copy-done.5), channel_id=1, replica_groups=mesh['prow'=4,'pcol'=8] {'pcol'}, dimensions={1}, use_global_device_ids=true | all-gather | bytes 147456 | tf_op jit(solution)/shard_map/all_gather | solution.py:39
  104.1 1.5 copy.63
  105.9 1.3 gather_fusion.2
  107.2 2.0 gather_fusion.4
  109.2 0.7 gather_fusion.6
  109.9 1.3 fusion.14
  111.4 40.7 %gather_fusion.11 = bf16[4096,256]{1,0:T(8,128)(2,1)} fusion(bf16[16,256,256]{2,1,0:T(8,128)(2,1)S(1)} %gather_fusion.6, s32[4096]{0:T(1024)S(1)} %bitcast.105), kind=kCustom, calls=%fused_computation.11 | custom fusion | bytes 4227072 | tf_op jit(solution)/shard_map/vmap()/gather | solution.py:19
  152.1 2.0 gather_fusion.3
  154.1 16.0 %copy_select_fusion = (bf16[16,256,256]{2,0,1:T(8,128)(2,1)}, bf16[16,256,256]{2,0,1:T(8,128)(2,1)S(1)}) fusion(bf16[16,256,256]{2,1,0:T(8,128)(2,1)} %gather_fusion.3, pred[16]{0:T(512)(128)(4,1)S(1)} %iota_compare_fusion.1, pred[16]{0:T(512)(128)(4,1)S(1)} %get-tuple-element.155, bf16[1,1,16,256,256]{4,3,2,1,0:T(8,128)(2,1)S(1)} %copy-done.1, ...), kind=kLoop, calls=%fused_computation.27 | loop fusion | flops 4194304 | bytes 12587056 | tf_op jit(solution)/shard_map/jit(_where)/select_n | solution.py:100
  170.1 2.1 copy.67
  172.2 2.2 gather_fusion.8
  174.4 2.1 copy.69
  176.5 2.2 gather_fusion.9
  178.7 1.0 broadcast_select_fusion.1
  179.7 1.3 sort.50
  181.0 0.7 convert_reduce_fusion
  181.8 2.4 scatter_fusion
  184.2 64.8 %all-reduce.4.cloned.1.call-done = bf16[3,256,256]{2,1,0:T(8,128)(2,1)} async-done(((bf16[3,256,256]{2,1,0:T(8,128)(2,1)}), bf16[3,256,256]{2,1,0:T(8,128)(2,1)}) %all-reduce.4.cloned.1.call-update) | async-done | bytes 393232 | tf_op jit(solution)/shard_map/psum | solution.py:15
  249.0 111.2 %while.11 = (s32[]{:T(128)}, bf16[16,256,256]{2,1,0:T(8,128)(2,1)}, s32[]{:T(128)}, s32[16]{0:T(128)S(1)}, bf16[16,256,256]{2,1,0:T(8,128)(2,1)}, /*index=5*/s32...) while((s32[]{:T(128)}, bf16[16,256,256]{2,1,0:T(8,128)(2,1)}, ...), condition=%wide.region_18.19_spmd, body=%wide.region_16.18_spmd.sunk | while | flops 33816608 | bytes 656726 | solution.py:117
  257.9 0.8 and_reduce_fusion.2
  258.7 2.6 fusion.49
  270.2 0.8 and_reduce_fusion.2
  271.0 2.6 fusion.49
  282.5 0.8 and_reduce_fusion.2
  283.3 2.6 fusion.49
  294.7 0.8 and_reduce_fusion.2
  295.5 2.6 fusion.49
  307.0 0.8 and_reduce_fusion.2
  307.8 2.6 fusion.49
  319.3 0.8 and_reduce_fusion.2
  320.1 2.6 fusion.49
  331.6 0.8 and_reduce_fusion.2
  332.4 2.6 fusion.49
  343.9 0.8 and_reduce_fusion.2
  344.7 2.6 fusion.49
  356.2 0.8 and_reduce_fusion.2
  356.9 2.6 fusion.49
  (95 shorter events, 21.7 us)
Async XLA Ops:
  6.5 97.5 %all-reduce.6.cloned.1.call-start = ((), (), s32[]{:S(2)}) async-start(), calls=%async_computation.1 | async-start | bytes 4194304 | tf_op jit(solution)/shard_map/psum | solution.py:54
  7.2 3.0 copy-start.8
  7.2 3.0 copy-start
  10.1 2.4 copy-start.7
  17.9 231.1 %all-reduce.4.cloned.1.call-start = ((), (), s32[]{:S(2)}) async-start(), calls=%async_computation | async-start | bytes 786432 | tf_op jit(solution)/shard_map/psum | solution.py:15
  43.9 23.4 %copy-start.4 = (bf16[64,256]{1,0:T(8,128)(2,1)S(1)}, bf16[64,256]{1,0:T(8,128)(2,1)}, u32[]{:S(2)}) copy-start(bf16[64,256]{1,0:T(8,128)(2,1)} %param.15) | copy-start | bytes 98308
  43.9 29.3 %copy-start.5 = (bf16[256,32]{0,1:T(8,128)(2,1)S(1)}, bf16[256,32]{0,1:T(8,128)(2,1)}, u32[]{:S(2)}) copy-start(bf16[256,32]{0,1:T(8,128)(2,1)} %param.14) | copy-start | bytes 49156
  104.1 1.5 copy-start.3
  152.1 2.0 copy-start.1
  170.1 4.3 %copy-start.2 = (bf16[16,256,256]{2,0,1:T(8,128)(2,1)S(1)}, bf16[16,256,256]{2,0,1:T(8,128)(2,1)}, u32[]{:S(2)}) copy-start(bf16[16,256,256]{2,0,1:T(8,128)(2,1)} %get-tuple-element.145) | copy-start | bytes 6291460
  176.5 72.5 %copy-start.6 = (s32[3]{0:T(128)S(1)}, s32[3]{0:T(128)}, u32[]{:S(2)}) copy-start(s32[3]{0:T(128)} %constant.108.clone.1) | copy-start | bytes 40
Sparse Core Ops, SparseCore 0:
  18.0 54.8 all-reduce.5
  179.8 69.1 all-reduce.3
where the time goes:
time: 369 us; the launch traced here: 367 us
  local copies, waits for them, and re-layouts  109 us (30%)
  waiting for transfers between devices  64.8 us (18%)
  loops' own time  62.9 us (17%)
  blocking collectives  56.7 us (15%)
  matrix products  30.7 us (8%)
  other arithmetic  28.2 us (8%)
  between operations  14.4 us (4%)
    psum x1, waiting for transfers between devices, broadcast(): return lax.psum(kept, axis)  64.8 us
    another operation x1, loops' own time, body(): result = lax.fori_loop(0, needed, own_step, result)  62.9 us
    gather x2, local copies, waits for them, and re-layouts, pick_rows(): return tile[rows]  40.7 us
    all_gather x1, blocking collectives, body(): lower_inv = lax.all_gather(l_inverse, 'pcol', axis=1, tiled=True)  30.7 us
    dot_general x9, matrix products, trailing(): jnp.dot(lower_tile, upper_list[upper_index], preferred_element_type=jnp.f...  23.2 us
    gather x1, local copies, waits for them, and re-layouts, body(): anchor = anchor_top[row_index]  23 us
    select_n x1, other arithmetic, body(): jnp.where(upper_mask[:, None, None], upper_list[upper_pick], result)  16 us
    dynamic_slice x18, local copies, waits for them, and re-layouts, own_step(): value = trailing(primed[slot], got_list[lower_pick[slot]], upper_pick[slot])  12.1 us
  transfers between devices with their start and end apart: 2, of which 1 were waited for; matrix products, arithmetic and copies ran while one was open for 9% of the time, Pallas kernels for 0%

commit v1 on v0

--- a/solution.py
+++ b/solution.py
@@ -8,6 +8,17 @@
 TILE_SLOTS = 16
 LOWER_MOST = 3
 UPPER_MOST = 3
+
+
+def gather_by_hops(x, mesh_axis, dim):
+    peers = lax.axis_size(mesh_axis)
+    hops = [(i, (i + 1) % peers) for i in range(peers)]
+    terms = [x]
+    for far in range(1, peers):
+        terms = [lax.ppermute(terms[0], mesh_axis, hops), *terms]
+    whole = jnp.concatenate(terms, axis=dim)
+    shift = (lax.axis_index(mesh_axis) + 1) * terms[-1].shape[dim]
+    return jnp.roll(whole, shift, axis=dim)
 
 
 def broadcast(value, axis, source):
@@ -36,7 +47,7 @@
     glob_col = my_col + col_count * loc_col
     col_range = jnp.arange(grid_cols, dtype=jnp.int32)
     upper_inv = lax.all_gather(u_inverse, "prow", axis=0, tiled=True)
-    lower_inv = lax.all_gather(l_inverse, "pcol", axis=1, tiled=True)
+    lower_inv = gather_by_hops(l_inverse, "pcol", 1)
     source_tile = pivots // TILE_SIDE
     source_row = pivots % TILE_SIDE
     gathered = local[:, source_row, :]

time: 369 us -> 379 us (1.027)
  waiting for transfers between devices: 64.8 us -> 103 us
  blocking collectives: 56.7 us -> 24 us
    ppermute x0 -> x7, waiting for transfers between devices: none -> 35.5 us  [gather_by_hops(): terms = [lax.ppermute(terms[0], mesh_axis, hops), *terms]]
    all_gather x1 -> x0, blocking collectives: 30.7 us -> none  [body(): lower_inv = lax.all_gather(l_inverse, 'pcol', axis=1, tiled=True)]
  transfers between devices with their start and end apart: 2 -> 9, of which waited for: 1 -> 7; matrix products, arithmetic and copies ran while one was open for 9% -> 12% of each run, Pallas kernels for 0% -> 0%
where the time goes in v1:
time: 379 us; the launch traced here: 378 us
  local copies, waits for them, and re-layouts  111 us (29%)
  waiting for transfers between devices  103 us (27%)
  loops' own time  62.9 us (17%)
  matrix products  30.8 us (8%)
  other arithmetic  28.2 us (7%)
  blocking collectives  24 us (6%)
  between operations  14.4 us (4%)
    psum x1, waiting for transfers between devices, broadcast(): return lax.psum(kept, axis)  67.9 us
    another operation x1, loops' own time, body(): result = lax.fori_loop(0, needed, own_step, result)  62.9 us
    gather x2, local copies, waits for them, and re-layouts, pick_rows(): return tile[rows]  40.7 us
    ppermute x7, waiting for transfers between devices, gather_by_hops(): terms = [lax.ppermute(terms[0], mesh_axis, hops), *terms]  35.5 us
    dot_general x9, matrix products, trailing(): jnp.dot(lower_tile, upper_list[upper_index], preferred_element_type=jnp.f...  23.2 us
    gather x1, local copies, waits for them, and re-layouts, body(): anchor = anchor_top[row_index]  23 us
    select_n x1, other arithmetic, body(): jnp.where(upper_mask[:, None, None], upper_list[upper_pick], result)  16 us
    dynamic_slice x18, local copies, waits for them, and re-layouts, own_step(): value = trailing(primed[slot], got_list[lower_pick[slot]], upper_pick[slot])  12.1 us
  transfers between devices with their start and end apart: 9, of which 7 were waited for; matrix products, arithmetic and copies ran while one was open for 12% of the time, Pallas kernels for 0%

profile of v1, /device:TPU:0, one launch (start us, length us, event | category | flops | bytes accessed | tf_op | source)
XLA Modules:
  0.0 377.8 jit_solution(14765433759952903598)
XLA Ops:
  6.5 0.8 copy.71
  7.4 3.0 collective-permute-start
  11.1 2.9 copy.102
  14.1 2.2 convolution_convert_fusion
  16.7 2.1 gather_fusion.1
  18.7 3.0 fusion.11
  21.8 6.3 %psum.35 = bf16[8]{0:T(256)(128)(2,1)S(1)} all-reduce(bf16[8]{0:T(256)(128)(2,1)S(1)} %multiply_reduce_fusion), channel_id=1, replica_groups=mesh['prow'=4,'pcol'=8] {'prow'}, use_global_device_ids=true, to_apply=%region_1.2 | all-reduce | flops 8 | bytes 32 | tf_op jit(solution)/shard_map/psum | solution.py:67
  28.1 1.0 sort.48
  29.8 1.2 sort.49
  32.4 11.6 %psum.38 = s32[3]{0:T(128)S(1)} all-reduce(s32[3]{0:T(128)S(1)} %broadcast_select_fusion.2), channel_id=1, replica_groups=mesh['prow'=4,'pcol'=8] {'pcol'}, use_global_device_ids=true, to_apply=%region_9.10 | all-reduce | flops 3 | bytes 24 | tf_op jit(solution)/shard_map/psum | solution.py:26
  44.2 1.4 scatter_custom_fusion
  45.7 23.0 %gather_fusion.5 = s32[4096]{0:T(1024)S(1)} fusion(s32[16384]{0:T(1024)S(1)} %scatter_custom_fusion, s32[4096]{0:T(1024)S(1)} %broadcast_clamp_fusion), kind=kCustom, calls=%fused_computation.5 | custom fusion | bytes 49152 | tf_op jit(solution)/shard_map/gather | solution.py:77
  69.2 6.7 %collective-permute-done.1 = bf16[256,32]{1,0:T(8,128)(2,1)S(1)} collective-permute-done((bf16[256,32]{1,0:T(8,128)(2,1)S(1)}, bf16[256,32]{1,0:T(8,128)(2,1)S(1)}, u32[]{:S(2)}, u32[]{:S(2)}) %collective-permute-start.1) | collective-permute-done | bytes 16416 | tf_op jit(solution)/shard_map/ppermute | solution.py:18
  76.0 6.9 %collective-permute-done.2 = bf16[256,32]{1,0:T(8,128)(2,1)S(1)} collective-permute-done((bf16[256,32]{1,0:T(8,128)(2,1)S(1)}, bf16[256,32]{1,0:T(8,128)(2,1)S(1)}, u32[]{:S(2)}, u32[]{:S(2)}) %collective-permute-start.2) | collective-permute-done | bytes 16416 | tf_op jit(solution)/shard_map/ppermute | solution.py:18
  82.8 7.3 %collective-permute-done.3 = bf16[256,32]{1,0:T(8,128)(2,1)S(1)} collective-permute-done((bf16[256,32]{1,0:T(8,128)(2,1)S(1)}, bf16[256,32]{1,0:T(8,128)(2,1)S(1)}, u32[]{:S(2)}, u32[]{:S(2)}) %collective-permute-start.3) | collective-permute-done | bytes 16416 | tf_op jit(solution)/shard_map/ppermute | solution.py:18
  90.2 7.0 %collective-permute-done.4 = bf16[256,32]{1,0:T(8,128)(2,1)S(1)} collective-permute-done((bf16[256,32]{1,0:T(8,128)(2,1)S(1)}, bf16[256,32]{1,0:T(8,128)(2,1)S(1)}, u32[]{:S(2)}, u32[]{:S(2)}) %collective-permute-start.4) | collective-permute-done | bytes 16416 | tf_op jit(solution)/shard_map/ppermute | solution.py:18
  97.1 7.0 %collective-permute-done.5 = bf16[256,32]{1,0:T(8,128)(2,1)S(1)} collective-permute-done((bf16[256,32]{1,0:T(8,128)(2,1)S(1)}, bf16[256,32]{1,0:T(8,128)(2,1)S(1)}, u32[]{:S(2)}, u32[]{:S(2)}) %collective-permute-start.5) | collective-permute-done | bytes 16416 | tf_op jit(solution)/shard_map/ppermute | solution.py:18
  104.1 6.0 %all_gather.3 = bf16[256,256]{1,0:T(8,128)(2,1)} all-gather(bf16[64,256]{1,0:T(8,128)(2,1)S(1)} %copy-done.5), channel_id=1, replica_groups=mesh['prow'=4,'pcol'=8] {'prow'}, dimensions={0}, use_global_device_ids=true | all-gather | bytes 163840 | tf_op jit(solution)/shard_map/all_gather | solution.py:49
  111.6 1.5 copy.78
  113.3 1.3 gather_fusion.2
  114.7 2.0 gather_fusion.4
  117.4 1.4 fusion.14
  118.9 40.7 %gather_fusion.11 = bf16[4096,256]{1,0:T(8,128)(2,1)} fusion(bf16[16,256,256]{2,1,0:T(8,128)(2,1)S(1)} %gather_fusion.6, s32[4096]{0:T(1024)S(1)} %bitcast.105), kind=kCustom, calls=%fused_computation.11 | custom fusion | bytes 4227072 | tf_op jit(solution)/shard_map/vmap()/gather | solution.py:30
  159.7 2.0 gather_fusion.3
  161.7 16.0 %copy_select_fusion = (bf16[16,256,256]{2,0,1:T(8,128)(2,1)}, bf16[16,256,256]{2,0,1:T(8,128)(2,1)S(1)}) fusion(bf16[16,256,256]{2,1,0:T(8,128)(2,1)} %gather_fusion.3, pred[16]{0:T(512)(128)(4,1)S(1)} %iota_compare_fusion.1, pred[16]{0:T(512)(128)(4,1)S(1)} %get-tuple-element.155, bf16[1,1,16,256,256]{4,3,2,1,0:T(8,128)(2,1)S(1)} %copy-done.1, ...), kind=kLoop, calls=%fused_computation.27 | loop fusion | flops 4194304 | bytes 12587056 | tf_op jit(solution)/shard_map/jit(_where)/select_n | solution.py:111
  177.7 2.1 copy.82
  179.8 2.2 gather_fusion.8
  182.0 2.1 copy.84
  184.1 2.2 gather_fusion.9
  186.2 1.0 broadcast_select_fusion.1
  187.3 1.3 sort.50
  189.4 2.4 scatter_fusion
  191.8 67.9 %all-reduce.4.cloned.1.call-done = bf16[3,256,256]{2,1,0:T(8,128)(2,1)} async-done(((bf16[3,256,256]{2,1,0:T(8,128)(2,1)}), bf16[3,256,256]{2,1,0:T(8,128)(2,1)}) %all-reduce.4.cloned.1.call-update) | async-done | bytes 393232 | tf_op jit(solution)/shard_map/psum | solution.py:26
  259.7 111.2 %while.11 = (s32[]{:T(128)}, bf16[16,256,256]{2,1,0:T(8,128)(2,1)}, s32[]{:T(128)}, s32[16]{0:T(128)S(1)}, bf16[16,256,256]{2,1,0:T(8,128)(2,1)}, /*index=5*/s32...) while((s32[]{:T(128)}, bf16[16,256,256]{2,1,0:T(8,128)(2,1)}, ...), condition=%wide.region_18.19_spmd, body=%wide.region_16.18_spmd.sunk | while | flops 33816608 | bytes 656726 | solution.py:128
  269.4 2.6 fusion.51
  281.7 2.6 fusion.51
  293.2 0.8 and_reduce_fusion.2
  294.0 2.6 fusion.51
  305.5 0.8 and_reduce_fusion.2
  306.3 2.6 fusion.51
  318.5 2.6 fusion.51
  330.8 2.6 fusion.51
  342.3 0.8 and_reduce_fusion.2
  343.1 2.6 fusion.51
  354.6 0.8 and_reduce_fusion.2
  355.4 2.6 fusion.51
  366.9 0.8 and_reduce_fusion.2
  367.7 2.6 fusion.51
  (110 shorter events, 27.8 us)
Async XLA Ops:
  6.5 105.0 %all-reduce.6.cloned.1.call-start = ((), (), s32[]{:S(2)}) async-start(), calls=%async_computation.1 | async-start | bytes 4194304 | tf_op jit(solution)/shard_map/psum | solution.py:65
  7.4 61.5 %collective-permute-start = (bf16[256,32]{1,0:T(8,128)(2,1)S(1)}, bf16[256,32]{1,0:T(8,128)(2,1)S(1)}, u32[]{:S(2)}, u32[]{:S(2)}) collective-permute-start(bf16[256,32]{1,0:T(8,128)(2,1)S(1)} %copy.71), channel_id=1, source_target_pairs={{0,1},{1,2},{2,3},{3,4},{4,5},{5,6},{6,7},{7,0},{8,9},{9,10},{10,1... | collective-permute-start | bytes 49160 | tf_op jit(solution)/shard_map/ppermute | solution.py:18
  11.1 3.0 copy-start.8
  11.1 3.0 copy-start
  14.0 2.4 copy-start.7
  21.7 238.0 %all-reduce.4.cloned.1.call-start = ((), (), s32[]{:S(2)}) async-start(), calls=%async_computation | async-start | bytes 786432 | tf_op jit(solution)/shard_map/psum | solution.py:26
  45.7 58.4 %copy-start.5 = (bf16[64,256]{1,0:T(8,128)(2,1)S(1)}, bf16[64,256]{1,0:T(8,128)(2,1)}, u32[]{:S(2)}) copy-start(bf16[64,256]{1,0:T(8,128)(2,1)} %param.15) | copy-start | bytes 98308
  68.9 7.0 %collective-permute-start.1 = (bf16[256,32]{1,0:T(8,128)(2,1)S(1)}, bf16[256,32]{1,0:T(8,128)(2,1)S(1)}, u32[]{:S(2)}, u32[]{:S(2)}) collective-permute-start(bf16[256,32]{1,0:T(8,128)(2,1)S(1)} %collective-permute-done), channel_id=1, source_target_pairs={{0,1},{1,2},{2,3},{3,4},{4,5},{5,6},{6,7},{7,0},{8,9},{9,10},{10,1... | collective-permute-start | bytes 49160 | tf_op jit(solution)/shard_map/ppermute | solution.py:18
  75.9 7.0 %collective-permute-start.2 = (bf16[256,32]{1,0:T(8,128)(2,1)S(1)}, bf16[256,32]{1,0:T(8,128)(2,1)S(1)}, u32[]{:S(2)}, u32[]{:S(2)}) collective-permute-start(bf16[256,32]{1,0:T(8,128)(2,1)S(1)} %collective-permute-done.1), channel_id=1, source_target_pairs={{0,1},{1,2},{2,3},{3,4},{4,5},{5,6},{6,7},{7,0},{8,9},{9,10},{10,1... | collective-permute-start | bytes 49160 | tf_op jit(solution)/shard_map/ppermute | solution.py:18
  82.8 7.3 %collective-permute-start.3 = (bf16[256,32]{1,0:T(8,128)(2,1)S(1)}, bf16[256,32]{1,0:T(8,128)(2,1)S(1)}, u32[]{:S(2)}, u32[]{:S(2)}) collective-permute-start(bf16[256,32]{1,0:T(8,128)(2,1)S(1)} %collective-permute-done.2), channel_id=1, source_target_pairs={{0,1},{1,2},{2,3},{3,4},{4,5},{5,6},{6,7},{7,0},{8,9},{9,10},{10,1... | collective-permute-start | bytes 49160 | tf_op jit(solution)/shard_map/ppermute | solution.py:18
  90.1 7.0 %collective-permute-start.4 = (bf16[256,32]{1,0:T(8,128)(2,1)S(1)}, bf16[256,32]{1,0:T(8,128)(2,1)S(1)}, u32[]{:S(2)}, u32[]{:S(2)}) collective-permute-start(bf16[256,32]{1,0:T(8,128)(2,1)S(1)} %collective-permute-done.3), channel_id=1, source_target_pairs={{0,1},{1,2},{2,3},{3,4},{4,5},{5,6},{6,7},{7,0},{8,9},{9,10},{10,1... | collective-permute-start | bytes 49160 | tf_op jit(solution)/shard_map/ppermute | solution.py:18
  97.1 7.0 %collective-permute-start.5 = (bf16[256,32]{1,0:T(8,128)(2,1)S(1)}, bf16[256,32]{1,0:T(8,128)(2,1)S(1)}, u32[]{:S(2)}, u32[]{:S(2)}) collective-permute-start(bf16[256,32]{1,0:T(8,128)(2,1)S(1)} %collective-permute-done.4), channel_id=1, source_target_pairs={{0,1},{1,2},{2,3},{3,4},{4,5},{5,6},{6,7},{7,0},{8,9},{9,10},{10,1... | collective-permute-start | bytes 49160 | tf_op jit(solution)/shard_map/ppermute | solution.py:18
  104.1 7.0 %collective-permute-start.6 = (bf16[256,32]{1,0:T(8,128)(2,1)S(1)}, bf16[256,32]{1,0:T(8,128)(2,1)S(1)}, u32[]{:S(2)}, u32[]{:S(2)}) collective-permute-start(bf16[256,32]{1,0:T(8,128)(2,1)S(1)} %collective-permute-done.5), channel_id=1, source_target_pairs={{0,1},{1,2},{2,3},{3,4},{4,5},{5,6},{6,7},{7,0},{8,9},{9,10},{10,1... | collective-permute-start | bytes 49160 | tf_op jit(solution)/shard_map/ppermute | solution.py:18
  111.6 1.5 copy-start.3
  159.7 2.0 copy-start.1
  177.7 4.3 %copy-start.2 = (bf16[16,256,256]{2,0,1:T(8,128)(2,1)S(1)}, bf16[16,256,256]{2,0,1:T(8,128)(2,1)}, u32[]{:S(2)}) copy-start(bf16[16,256,256]{2,0,1:T(8,128)(2,1)} %get-tuple-element.145) | copy-start | bytes 6291460
  182.0 4.3 %copy-start.4 = (bf16[256,256]{1,0:T(8,128)(2,1)S(1)}, bf16[256,256]{1,0:T(8,128)(2,1)}, u32[]{:S(2)}) copy-start(bf16[256,256]{1,0:T(8,128)(2,1)} %all_gather.3) | copy-start | bytes 393220
  184.1 75.6 %copy-start.6 = (s32[3]{0:T(128)S(1)}, s32[3]{0:T(128)}, u32[]{:S(2)}) copy-start(s32[3]{0:T(128)} %constant.124.clone.1) | copy-start | bytes 40
Sparse Core Ops, SparseCore 0:
  21.9 51.7 all-reduce.5
  187.4 72.2 all-reduce.3
